TPU v7x, 32 devices: a whole 2x2x4 slice. The times are simulated.
32 devices in a mesh: grp: 1, sp: 32 (over z, y, x, core), ch: 1.
Axes of the slice: x: 2, y: 2, z: 4, core: 2. Of those that a mesh axis runs over, the one named last changes fastest.
Arguments:
- latents: bfloat16 [131072, 1024], P(('grp', 'sp')), may hold values from -6 to 6
- spectrum: bfloat16 [16, 64, 128, 1024], P(None, None, 'sp', 'ch'), may hold values from -4 to 4
- w_value: bfloat16 [1024, 1024], P('sp', 'ch'), may hold values from -0.1875 to 0.1875
- w_gate: bfloat16 [1024, 1024], P('sp', 'ch'), may hold values from -0.1875 to 0.1875
- w_out: bfloat16 [1024, 1024], P('sp'), may hold values from -0.1875 to 0.1875
- embed_table: bfloat16 [1024, 32768], P(('sp', 'ch')), may hold values from -12 to 12
- prompt_ids: int32 [256], P('grp'), may hold values from 0 to 32767
- noise_step: int32 [1], P('grp'), may hold values from 0 to 999
Outputs:
- denoised: bfloat16 [131072, 1024], P(('grp', 'sp', 'ch'))
All inputs are finite; a program needn't handle non-finite values.
Results may differ from a plain program's by a relative error of at most 0.013.
Values may be sent and summed in bfloat16 or wider, within the bound.
No kernel may reach another device: no remote copies, remote signals or barrier semaphores. Data moves between devices by JAX's collectives and lax.ppermute only.
A program may use at most 128 MiB of HBM per device.

v0:
```python
import math
import jax
import jax.numpy as jnp
from jax import lax
from jax.sharding import PartitionSpec as P

TT = 16
HH = 64
WW = 128
C = 1024


def cas_table(length):
    position = jnp.arange(length, dtype=jnp.int32)
    product = position[:, None] * position[None, :] % length
    phase_angle = product.astype(jnp.float32) * (2.0 * math.pi / length)
    return ((jnp.cos(phase_angle) + jnp.sin(phase_angle)) / math.sqrt(length)).astype(jnp.bfloat16)


def step_embedding(noise_step, channel, channels):
    half_count = channels // 2
    lower_half = channel < half_count
    position = jnp.where(lower_half, channel, channel - half_count).astype(jnp.float32)
    frequency = jnp.exp(-math.log(10000.0) * position / half_count)
    phase_angle = noise_step[0].astype(jnp.float32) * frequency
    return jnp.where(lower_half, jnp.sin(phase_angle), jnp.cos(phase_angle))


def apply_table(form, table, operand):
    return jnp.einsum(form, table, operand, preferred_element_type=jnp.float32)


def local(latents, spectrum, w_value, w_gate, w_out, embed_table, prompt_ids, noise_step):
    row_count = latents.shape[0]
    chan_part = w_value.shape[1]
    full_value, full_gate, full_out = (
        lax.all_gather(w_value, "sp", axis=0, tiled=True),
        lax.all_gather(w_gate, "sp", axis=0, tiled=True),
        lax.all_gather(w_out, "sp", axis=0, tiled=True),
    )
    value_rows = jnp.dot(latents, full_value, preferred_element_type=jnp.float32).astype(
        jnp.bfloat16
    )
    gate_rows = jnp.dot(latents, full_gate, preferred_element_type=jnp.float32)
    cas_width = cas_table(WW)
    cas_height = cas_table(HH)
    cas_time = cas_table(TT)
    line_grid = value_rows.reshape(row_count // WW, WW, chan_part)
    width_spec = apply_table("kw,lwc->lkc", cas_width, line_grid).astype(jnp.bfloat16)
    pencil = lax.all_to_all(width_spec, "sp", split_axis=1, concat_axis=0, tiled=True)
    band_count = pencil.shape[1]
    pencil = pencil.reshape(TT, HH, band_count, chan_part)
    height_spec = apply_table("ah,thkc->takc", cas_height, pencil).astype(jnp.bfloat16)
    full_spec = apply_table("st,takc->sakc", cas_time, height_spec).astype(jnp.bfloat16)
    filtered = (full_spec.astype(jnp.float32) * spectrum.astype(jnp.float32)).astype(jnp.bfloat16)
    time_back = apply_table("ts,sakc->takc", cas_time, filtered).astype(jnp.bfloat16)
    height_back = apply_table("ha,takc->thkc", cas_height, time_back).astype(jnp.bfloat16)
    returned = lax.all_to_all(
        height_back.reshape(TT * HH, band_count, chan_part),
        "sp",
        split_axis=0,
        concat_axis=1,
        tiled=True,
    )
    mix_rows = apply_table("wk,lkc->lwc", cas_width, returned).reshape(row_count, chan_part)
    offset = lax.axis_index("ch") * chan_part
    local_pool = jnp.mean(jnp.take(embed_table, prompt_ids, axis=1).astype(jnp.float32), axis=1)
    pooled_all = lax.all_gather(local_pool, ("sp", "ch"), axis=0, tiled=True)
    pooled = lax.dynamic_slice_in_dim(pooled_all, offset, chan_part)
    channel = offset + jnp.arange(chan_part, dtype=jnp.int32)
    modulation = 1.0 + pooled + step_embedding(noise_step, channel, C)
    mixed_rows = (mix_rows * jax.nn.silu(gate_rows) * modulation[None, :]).astype(jnp.bfloat16)
    half_rows = row_count // lax.axis_size("ch")
    own_rows = lax.dynamic_slice_in_dim(full_out, offset, chan_part, 0)
    summed = lax.psum_scatter(
        jnp.dot(mixed_rows, own_rows, preferred_element_type=jnp.float32).astype(jnp.bfloat16),
        "ch",
        scatter_dimension=0,
        tiled=True,
    ).astype(jnp.float32)
    residual = lax.dynamic_slice_in_dim(latents, lax.axis_index("ch") * half_rows, half_rows, 0)
    return (residual.astype(jnp.float32) + summed).astype(jnp.bfloat16)


def solution(mesh):
    placed = (
        P(("grp", "sp"), None),
        P(None, None, "sp", "ch"),
        P("sp", "ch"),
        P("sp", "ch"),
        P("sp", None),
        P(("sp", "ch"), None),
        P("grp"),
        P("grp"),
    )
    return jax.shard_map(
        local, mesh=mesh, in_specs=placed, out_specs=P(("grp", "sp", "ch"), None), check_vma=False
    )
```

profile of v0, /device:TPU:0, one launch (start us, length us, event | category | flops | bytes accessed | tf_op | source)
XLA Modules:
  0.0 686.7 jit_solution(4367004813713135409)
XLA Ops:
  6.5 0.0 all-gather.4.cloned.1.call-start
  6.5 0.7 all-gather.4.cloned.1.call-update
  7.3 61.9 %all-gather.4.cloned.1.call-done = bf16[1024,1024]{1,0:T(8,128)(2,1)} async-done(((bf16[32,1024]{1,0:T(8,128)(2,1)}), bf16[1024,1024]{1,0:T(8,128)(2,1)}) %all-gather.4.cloned.1.call-update) | async-done | bytes 2097168 | tf_op jit(solution)/shard_map/all_gather | solution.py:37
  69.1 12.8 %convolution_convert_fusion = bf16[4096,1024]{1,0:T(8,128)(2,1)S(1)} fusion(bf16[4096,1024]{1,0:T(8,128)(2,1)} %param.8, bf16[1024,1024]{1,0:T(8,128)(2,1)} %all-gather.4.cloned.1.call-done), kind=kOutput, calls=%fused_computation.18 | convolution fusion | flops 8594128896 | bytes 18874368 | tf_op jit(solution)/shard_map/dot_general | solution.py:41
  82.0 5.1 convert_bitcast_fusion.2
  87.1 12.4 %copy.18 = bf16[32,128,1024]{2,0,1:T(8,128)(2,1)} copy(bf16[32,128,1024]{1,2,0:T(8,128)(2,1)} %convert_bitcast_fusion.2) | data formatting | bytes 16777216 | tf_op jit(solution)/shard_map/convert_element_type | solution.py:49
  99.5 187.2 %all_to_all.33 = bf16[32,128,1024]{2,0,1:T(8,128)(2,1)} all-to-all(bf16[32,128,1024]{2,0,1:T(8,128)(2,1)} %copy.18), channel_id=1, replica_groups=mesh['grp'=1,'sp'=32,'ch'=1] {'sp'}, dimensions={1} | all-to-all | bytes 16777216 | tf_op jit(solution)/shard_map/all_to_all | solution.py:50
  286.7 8.6 %copy.19 = bf16[32,32,4,1024]{3,1,0,2:T(8,128)(2,1)} copy(bf16[32,32,4,1024]{3,1,2,0:T(8,128)(2,1)} %bitcast.48) | data formatting | bytes 16777216 | tf_op jit(solution)/shard_map/all_to_all | solution.py:50
  295.4 9.1 %convert_bitcast_fusion.1 = bf16[16,64,4,1024]{3,1,2,0:T(8,128)(2,1)} fusion(bf16[16,64,4,1024]{3,1,0,2:T(8,128)(2,1)} %bitcast.49), kind=kOutput, calls=%fused_computation.16 | convolution fusion | flops 541134848 | bytes 16777216 | tf_op jit(solution)/shard_map/ah,thkc->takc/dot_general | solution.py:30
  304.4 26.6 %fusion.15 = bf16[16,64,4,1024]{3,0,2,1:T(8,128)(2,1)} fusion(bf16[16,64,4,1024]{3,2,1,0:T(4,128)(2,1)} %param.9, bf16[16,64,4,1024]{3,1,2,0:T(8,128)(2,1)} %convert_bitcast_fusion.1), kind=kOutput, calls=%fused_computation.19 | convolution fusion | flops 293609984 | bytes 25165824 | tf_op jit(solution)/shard_map/ts,sakc->takc/dot_general | solution.py:30
  331.1 17.6 %convert_bitcast_fusion = bf16[16,64,4,1024]{3,1,2,0:T(8,128)(2,1)} fusion(bf16[16,64,4,1024]{3,0,2,1:T(8,128)(2,1)} %fusion.15), kind=kOutput, calls=%fused_computation.14 | convolution fusion | flops 541134848 | bytes 16777216 | tf_op jit(solution)/shard_map/ha,takc->thkc/dot_general | solution.py:30
  348.7 8.6 %copy.24 = bf16[16,64,4,1024]{3,1,0,2:T(8,128)(2,1)} copy(bf16[16,64,4,1024]{3,1,2,0:T(8,128)(2,1)} %convert_bitcast_fusion) | data formatting | bytes 16777216 | tf_op jit(solution)/shard_map/convert_element_type | solution.py:57
  357.2 12.5 %copy.25 = bf16[1024,4,1024]{2,1,0:T(4,128)(2,1)} copy(bf16[1024,4,1024]{2,0,1:T(8,128)(2,1)} %bitcast.50) | data formatting | bytes 16777216 | tf_op jit(solution)/shard_map/reshape | solution.py:59
  369.8 3.8 all-to-all-start.1
  373.6 0.0 copy-start.1
  373.6 0.0 all-gather.6.cloned.1.call-start
  373.7 0.7 all-gather.6.cloned.1.call-update
  374.4 0.0 all-gather.8.cloned.1.call-start
  374.4 0.7 all-gather.8.cloned.1.call-update
  375.1 0.0 copy-done
  375.1 5.9 copy.28
  381.7 5.2 gather_fusion
  386.9 0.1 convert_reduce_fusion
  387.0 0.1 multiply_dynamic-update-slice_fusion
  387.2 210.4 %all-reduce = f32[1024]{0:T(1024)S(1)} all-reduce(f32[1024]{0:T(1024)S(1)} %multiply_dynamic-update-slice_fusion), channel_id=1, replica_groups=mesh['grp'=1,'sp'=32,'ch'=1] {'sp','ch'}, use_global_device_ids=true, to_apply=%add | all-reduce | flops 1024 | bytes 8192
  597.6 0.0 all-to-all-done.1
  597.6 9.6 %copy.26 = bf16[1024,4,1024]{2,0,1:T(8,128)(2,1)} copy(bf16[1024,4,1024]{2,1,0:T(4,128)(2,1)} %all-to-all-done.1) | data formatting | bytes 16777216 | tf_op jit(solution)/shard_map/all_to_all | solution.py:58
  607.2 12.2 %copy.27 = bf16[32,32,4,1024]{3,2,1,0:T(4,128)(2,1)} copy(bf16[32,32,4,1024]{3,0,1,2:T(8,128)(2,1)} %bitcast.51) | data formatting | bytes 16777216 | tf_op jit(solution)/shard_map/all_to_all | solution.py:58
  619.4 12.5 %all_to_all.30 = bf16[32,128,1024]{2,1,0:T(8,128)(2,1)} reshape(bf16[32,32,4,1024]{3,2,1,0:T(4,128)(2,1)} %copy.27) | data formatting | bytes 16777216 | tf_op jit(solution)/shard_map/all_to_all | solution.py:58
  631.9 11.7 %fusion.32 = f32[32,1024,128]{1,2,0:T(8,128)} fusion(bf16[32,128,1024]{2,1,0:T(8,128)(2,1)} %all_to_all.30), kind=kOutput, calls=%fused_computation.41 | convolution fusion | flops 1074020352 | bytes 25165824 | tf_op jit(solution)/shard_map/wk,lkc->lwc/dot_general | solution.py:30
  643.6 20.4 %fusion.1 = bf16[4096,1024]{1,0:T(8,128)(2,1)} fusion(f32[32,1024,128]{1,2,0:T(8,128)} %fusion.32, f32[1024]{0:T(1024)S(1)} %select_add_fusion, bf16[4096,1024]{1,0:T(8,128)(2,1)} %param.8, bf16[1024,1024]{1,0:T(8,128)(2,1)} %all-gather.6.cloned.1.call-done), kind=kOutput, calls=%fused_computation.3 | convolution fusion | flops 8619294720 | bytes 35655680 | tf_op jit(solution)/shard_map/dot_general | solution.py:44
  663.9 16.1 %add_convert_fusion = bf16[4096,1024]{1,0:T(8,128)(2,1)} fusion(bf16[4096,1024]{1,0:T(8,128)(2,1)} %param.8, bf16[4096,1024]{1,0:T(8,128)(2,1)} %fusion.1, bf16[1024,1024]{1,0:T(8,128)(2,1)} %all-gather.8.cloned.1.call-done), kind=kOutput, calls=%fused_computation.4 | convolution fusion | flops 8610906112 | bytes 27262976 | tf_op jit(solution)/shard_map/dot_general | solution.py:76
  (9 shorter events, 0.1 us)
Async XLA Ops:
  6.5 62.6 %all-gather.4.cloned.1.call-start = ((), (), s32[]{:S(2)}) async-start(), calls=%async_computation.2 | async-start | bytes 2162688 | tf_op jit(solution)/shard_map/all_gather | solution.py:37
  369.8 5.3 copy-start
  369.8 227.8 %all-to-all-start.1 = ((bf16[1024,4,1024]{2,1,0:T(4,128)(2,1)}), bf16[1024,4,1024]{2,1,0:T(4,128)(2,1)}, u32[]{:S(2)}, u32[]{:S(2)}) async-start(bf16[1024,4,1024]{2,1,0:T(4,128)(2,1)} %copy.25), calls=%async_computation.1 | async-start | bytes 16777216 | tf_op jit(solution)/shard_map/all_to_all | solution.py:58
  373.6 8.1 %copy-start.1 = (s32[256]{0:T(256)S(1)}, s32[256]{0:T(256)}, u32[]{:S(2)}) copy-start(s32[256]{0:T(256)} %param.14) | copy-start | bytes 3076
  373.6 270.0 %all-gather.6.cloned.1.call-start = ((), (), s32[]{:S(2)}) async-start(), calls=%async_computation.3 | async-start | bytes 2162688 | tf_op jit(solution)/shard_map/all_gather | solution.py:38
  374.4 289.6 %all-gather.8.cloned.1.call-start = ((), (), s32[]{:S(2)}) async-start(), calls=%async_computation.4 | async-start | bytes 2162688 | tf_op jit(solution)/shard_map/all_gather | solution.py:39
Sparse Core Ops, SparseCore 0:
  10.2 58.9 all-gather.3
  377.3 96.9 all-gather.5
  477.2 78.9 all-gather.7
where the time goes:
time: 695 us; the launch traced here: 687 us
  blocking collectives  398 us (57%)
  matrix products  119 us (17%)
  local copies, waits for them, and re-layouts  87.6 us (13%)
  waiting for transfers between devices  64 us (9%)
  between operations  14 us (2%)
    unnamed x1, blocking collectives  210 us
    all_to_all x1, blocking collectives, local(): lax.all_to_all(width_spec, 'sp', split_axis=1, concat_axis=0, tiled=True)  187 us
    dot_general x5, matrix products, apply_table(): return jnp.einsum(form, table, operand, preferred_element_type=jnp.float32)  70.1 us
    all_gather x1, waiting for transfers between devices, local(): lax.all_gather(w_value, 'sp', axis=0, tiled=True)  61.9 us
    all_to_all x3, local copies, waits for them, and re-layouts, local(): lax.all_to_all(height_back.reshape(TT * HH, band_count, chan_part), 'sp',...  34.3 us
    dot_general x1, matrix products, local(): gate_rows = jnp.dot(latents, full_gate, preferred_element_type=jnp.float32)  20.4 us
    dot_general x1, matrix products, local(): jnp.dot(mixed_rows, own_rows, preferred_element_type=jnp.float32)  16.1 us
  transfers between devices with their start and end apart: 4, of which 1 were waited for; matrix products, arithmetic and copies ran while one was open for 10% of the time, Pallas kernels for 0%

commit v1 on v0

--- a/solution.py
+++ b/solution.py
@@ -47,7 +47,9 @@
     cas_time = cas_table(TT)
     line_grid = value_rows.reshape(row_count // WW, WW, chan_part)
     width_spec = apply_table("kw,lwc->lkc", cas_width, line_grid).astype(jnp.bfloat16)
-    pencil = lax.all_to_all(width_spec, "sp", split_axis=1, concat_axis=0, tiled=True)
+    pieces = jnp.split(width_spec, lax.axis_size("sp"), axis=1)
+    received = lax.all_to_all(jnp.stack(pieces), "sp", 0, 0)
+    pencil = jnp.concatenate(received, axis=0)
     band_count = pencil.shape[1]
     pencil = pencil.reshape(TT, HH, band_count, chan_part)
     height_spec = apply_table("ah,thkc->takc", cas_height, pencil).astype(jnp.bfloat16)

time: 695 us -> 672 us (0.967)
  local copies, waits for them, and re-layouts: 87.6 us -> 70.7 us
    convert_element_type x1 -> x0, local copies, waits for them, and re-layouts: 12.4 us -> none  [local(): apply_table('kw,lwc->lkc', cas_width, line_grid).astype(jnp.bfloat16)]
    all_to_all x1 -> x0, local copies, waits for them, and re-layouts: 8.64 us -> none  [local(): lax.all_to_all(width_spec, 'sp', split_axis=1, concat_axis=0, tiled=True)]
where the time goes in v1:
time: 672 us; the launch traced here: 664 us
  blocking collectives  397 us (59%)
  matrix products  113 us (17%)
  local copies, waits for them, and re-layouts  70.7 us (11%)
  waiting for transfers between devices  64 us (10%)
  between operations  14.2 us (2%)
    unnamed x1, blocking collectives  210 us
    all_to_all x1, blocking collectives, local(): received = lax.all_to_all(jnp.stack(pieces), 'sp', 0, 0)  187 us
    dot_general x5, matrix products, apply_table(): return jnp.einsum(form, table, operand, preferred_element_type=jnp.float32)  64.2 us
    all_gather x1, waiting for transfers between devices, local(): lax.all_gather(w_value, 'sp', axis=0, tiled=True)  61.9 us
    all_to_all x3, local copies, waits for them, and re-layouts, local(): lax.all_to_all(height_back.reshape(TT * HH, band_count, chan_part), 'sp',...  34.3 us
    dot_general x1, matrix products, local(): gate_rows = jnp.dot(latents, full_gate, preferred_element_type=jnp.float32)  20.4 us
    dot_general x1, matrix products, local(): jnp.dot(mixed_rows, own_rows, preferred_element_type=jnp.float32)  16.1 us
  transfers between devices with their start and end apart: 4, of which 1 were waited for; matrix products, arithmetic and copies ran while one was open for 10% of the time, Pallas kernels for 0%

profile of v1, /device:TPU:0, one launch (start us, length us, event | category | flops | bytes accessed | tf_op | source)
XLA Modules:
  0.0 663.8 jit_solution(13410024349637824087)
XLA Ops:
  6.5 0.7 all-gather.4.cloned.1.call-update
  7.3 61.9 %all-gather.4.cloned.1.call-done = bf16[1024,1024]{1,0:T(8,128)(2,1)} async-done(((bf16[32,1024]{1,0:T(8,128)(2,1)}), bf16[1024,1024]{1,0:T(8,128)(2,1)}) %all-gather.4.cloned.1.call-update) | async-done | bytes 2097168 | tf_op jit(solution)/shard_map/all_gather | solution.py:37
  69.1 12.8 %convolution_convert_fusion = bf16[4096,1024]{1,0:T(8,128)(2,1)S(1)} fusion(bf16[4096,1024]{1,0:T(8,128)(2,1)} %param.8, bf16[1024,1024]{1,0:T(8,128)(2,1)} %all-gather.4.cloned.1.call-done), kind=kOutput, calls=%fused_computation.18 | convolution fusion | flops 8594128896 | bytes 18874368 | tf_op jit(solution)/shard_map/dot_general | solution.py:41
  82.0 2.6 convert_bitcast_fusion.2
  84.6 0.2 fusion.50
  84.9 0.2 fusion.48
  85.5 0.2 fusion.44
  86.0 0.2 fusion.40
  86.3 0.2 fusion.38
  86.9 0.2 fusion.34
  87.1 0.2 fusion.32
  87.7 0.2 fusion.28
  88.0 0.2 fusion.26
  88.3 0.2 fusion.24
  89.0 186.9 %all_to_all.23 = bf16[32,32,4,1024]{3,2,1,0:T(4,128)(2,1)S(1)} all-to-all(bf16[32,32,4,1024]{3,2,1,0:T(4,128)(2,1)S(1)} %fusion.20), channel_id=1, replica_groups=mesh['grp'=1,'sp'=32,'ch'=1] {'sp'}, dimensions={0} | all-to-all | bytes 16777216 | tf_op jit(solution)/shard_map/all_to_all | solution.py:51
  275.9 5.7 convert_bitcast_fusion.1
  281.6 26.5 %fusion.15 = bf16[16,64,4,1024]{3,0,2,1:T(8,128)(2,1)} fusion(bf16[16,64,4,1024]{3,2,1,0:T(4,128)(2,1)} %param.9, bf16[16,64,4,1024]{3,1,2,0:T(8,128)(2,1)} %convert_bitcast_fusion.1), kind=kOutput, calls=%fused_computation.19 | convolution fusion | flops 293609984 | bytes 25165824 | tf_op jit(solution)/shard_map/ts,sakc->takc/dot_general | solution.py:30
  308.1 17.7 %convert_bitcast_fusion = bf16[16,64,4,1024]{3,1,2,0:T(8,128)(2,1)} fusion(bf16[16,64,4,1024]{3,0,2,1:T(8,128)(2,1)} %fusion.15), kind=kOutput, calls=%fused_computation.14 | convolution fusion | flops 541134848 | bytes 16777216 | tf_op jit(solution)/shard_map/ha,takc->thkc/dot_general | solution.py:30
  325.8 8.4 %copy.17 = bf16[16,64,4,1024]{3,1,0,2:T(8,128)(2,1)} copy(bf16[16,64,4,1024]{3,1,2,0:T(8,128)(2,1)} %convert_bitcast_fusion) | data formatting | bytes 16777216 | tf_op jit(solution)/shard_map/convert_element_type | solution.py:59
  334.3 12.5 %copy.18 = bf16[1024,4,1024]{2,1,0:T(4,128)(2,1)} copy(bf16[1024,4,1024]{2,0,1:T(8,128)(2,1)} %bitcast.174) | data formatting | bytes 16777216 | tf_op jit(solution)/shard_map/reshape | solution.py:61
  346.8 3.9 all-to-all-start.1
  350.7 0.7 all-gather.6.cloned.1.call-update
  351.5 0.7 all-gather.8.cloned.1.call-update
  352.2 6.0 copy.21
  358.9 5.2 gather_fusion
  364.3 210.3 %all-reduce = f32[1024]{0:T(1024)S(1)} all-reduce(f32[1024]{0:T(1024)S(1)} %multiply_dynamic-update-slice_fusion), channel_id=1, replica_groups=mesh['grp'=1,'sp'=32,'ch'=1] {'sp','ch'}, use_global_device_ids=true, to_apply=%add | all-reduce | flops 1024 | bytes 8192
  574.7 9.6 %copy.19 = bf16[1024,4,1024]{2,0,1:T(8,128)(2,1)} copy(bf16[1024,4,1024]{2,1,0:T(4,128)(2,1)} %all-to-all-done.1) | data formatting | bytes 16777216 | tf_op jit(solution)/shard_map/all_to_all | solution.py:60
  584.3 12.2 %copy.20 = bf16[32,32,4,1024]{3,2,1,0:T(4,128)(2,1)} copy(bf16[32,32,4,1024]{3,0,1,2:T(8,128)(2,1)} %bitcast.175) | data formatting | bytes 16777216 | tf_op jit(solution)/shard_map/all_to_all | solution.py:60
  596.5 12.5 %all_to_all.20 = bf16[32,128,1024]{2,1,0:T(8,128)(2,1)} reshape(bf16[32,32,4,1024]{3,2,1,0:T(4,128)(2,1)} %copy.20) | data formatting | bytes 16777216 | tf_op jit(solution)/shard_map/all_to_all | solution.py:60
  608.9 11.7 %fusion.65 = f32[32,1024,128]{1,2,0:T(8,128)} fusion(bf16[32,128,1024]{2,1,0:T(8,128)(2,1)} %all_to_all.20), kind=kOutput, calls=%fused_computation.105 | convolution fusion | flops 1074020352 | bytes 25165824 | tf_op jit(solution)/shard_map/wk,lkc->lwc/dot_general | solution.py:30
  620.6 20.4 %fusion.1 = bf16[4096,1024]{1,0:T(8,128)(2,1)} fusion(f32[32,1024,128]{1,2,0:T(8,128)} %fusion.65, f32[1024]{0:T(1024)S(1)} %select_add_fusion, bf16[4096,1024]{1,0:T(8,128)(2,1)} %param.8, bf16[1024,1024]{1,0:T(8,128)(2,1)} %all-gather.6.cloned.1.call-done), kind=kOutput, calls=%fused_computation.3 | convolution fusion | flops 8619294720 | bytes 35655680 | tf_op jit(solution)/shard_map/dot_general | solution.py:44
  641.0 16.1 %add_convert_fusion = bf16[4096,1024]{1,0:T(8,128)(2,1)} fusion(bf16[4096,1024]{1,0:T(8,128)(2,1)} %param.8, bf16[4096,1024]{1,0:T(8,128)(2,1)} %fusion.1, bf16[1024,1024]{1,0:T(8,128)(2,1)} %all-gather.8.cloned.1.call-done), kind=kOutput, calls=%fused_computation.4 | convolution fusion | flops 8610906112 | bytes 27262976 | tf_op jit(solution)/shard_map/dot_general | solution.py:78
  (39 shorter events, 3.1 us)
Async XLA Ops:
  6.5 62.6 %all-gather.4.cloned.1.call-start = ((), (), s32[]{:S(2)}) async-start(), calls=%async_computation.2 | async-start | bytes 2162688 | tf_op jit(solution)/shard_map/all_gather | solution.py:37
  346.8 5.4 copy-start
  346.8 227.9 %all-to-all-start.1 = ((bf16[1024,4,1024]{2,1,0:T(4,128)(2,1)}), bf16[1024,4,1024]{2,1,0:T(4,128)(2,1)}, u32[]{:S(2)}, u32[]{:S(2)}) async-start(bf16[1024,4,1024]{2,1,0:T(4,128)(2,1)} %copy.18), calls=%async_computation.1 | async-start | bytes 16777216 | tf_op jit(solution)/shard_map/all_to_all | solution.py:60
  350.7 8.2 %copy-start.1 = (s32[256]{0:T(256)S(1)}, s32[256]{0:T(256)}, u32[]{:S(2)}) copy-start(s32[256]{0:T(256)} %param.14) | copy-start | bytes 3076
  350.7 269.9 %all-gather.6.cloned.1.call-start = ((), (), s32[]{:S(2)}) async-start(), calls=%async_computation.3 | async-start | bytes 2162688 | tf_op jit(solution)/shard_map/all_gather | solution.py:38
  351.5 289.5 %all-gather.8.cloned.1.call-start = ((), (), s32[]{:S(2)}) async-start(), calls=%async_computation.4 | async-start | bytes 2162688 | tf_op jit(solution)/shard_map/all_gather | solution.py:39
Sparse Core Ops, SparseCore 0:
  10.2 58.9 all-gather.3
  354.4 96.9 all-gather.5
  454.3 78.9 all-gather.7
